TPU v7x, 32 devices: a whole 2x2x4 slice. The times are simulated.
32 devices in a mesh: cand: 4 (over y, core), tensor: 8 (over z, x).
Axes of the slice: x: 2, y: 2, z: 4, core: 2. Of those that a mesh axis runs over, the one named last changes fastest.
Arguments:
- states: bfloat16 [512, 3584], P('cand'), may hold values from -60 to 60
- targets: int32 [512], replicated, may hold values from 0 to 131071
- loss_mask: int32 [512], P('cand'), may hold values 0 or 1
- cand_of: int32 [4], replicated, may hold values from 0 to 3
- lambdas: float32 [4], replicated, may hold values from 0.2 to 1
- base_q: bfloat16 [3584, 4096], P('cand', 'tensor'), may hold values from -0.09375 to 0.09375
- delta_q: bfloat16 [2, 3584, 4096], P(None, 'cand', 'tensor'), may hold values from -0.046875 to 0.046875
- base_k: bfloat16 [3584, 2048], P('cand'), may hold values from -0.09375 to 0.09375
- delta_k: bfloat16 [2, 3584, 2048], P(None, 'cand'), may hold values from -0.046875 to 0.046875
- base_v: bfloat16 [3584, 2048], P('cand'), may hold values from -0.09375 to 0.09375
- delta_v: bfloat16 [2, 3584, 2048], P(None, 'cand'), may hold values from -0.046875 to 0.046875
- base_o: bfloat16 [4096, 3584], P('tensor', 'cand'), may hold values from -0.09375 to 0.09375
- delta_o: bfloat16 [2, 4096, 3584], P(None, 'tensor', 'cand'), may hold values from -0.046875 to 0.046875
- pre_gain: float32 [3584], replicated, may hold values from 0.5 to 2
- post_gain: float32 [3584], replicated, may hold values from 0.5 to 2
- final_gain: float32 [3584], replicated, may hold values from 0.5 to 2
- unembed: bfloat16 [3584, 131072], P(None, ('cand', 'tensor')), may hold values from -0.3125 to 0.3125
Outputs:
- token_loss: float32 [512], P('cand')
- cand_loss: float32 [4], replicated
All inputs are finite; a program needn't handle non-finite values. No bound on the sum of `loss_mask` on one device may be relied on, other than what follows from the above.
Results may differ from a plain program's by a relative error of at most 0.002.
Values may be sent and summed in bfloat16 or wider, within the bound.
No kernel may reach another device: no remote copies, remote signals or barrier semaphores. Data moves between devices by JAX's collectives and lax.ppermute only.
A program may use at most 128 MiB of HBM per device.

v0:
```python
import math
import jax
import jax.numpy as jnp
from jax import lax
from jax.sharding import PartitionSpec as P

KV = 8
HEAD_SIZE = 256
CANDS = 4


def root_norm(entries, scale_gain):
    mean_square = jnp.mean(entries * entries, axis=-1, keepdims=True)
    return entries * lax.rsqrt(mean_square + 1e-06) * scale_gain


def rotate_pairs(entries, length):
    half_width = entries.shape[-1] // 2
    positions = jnp.arange(length).astype(jnp.float32)
    frequency = jnp.exp(
        -math.log(10000.0) * jnp.arange(half_width).astype(jnp.float32) * 2.0 / entries.shape[-1]
    )
    angles = positions[:, None] * frequency[None, :]
    cosine = jnp.cos(angles)[:, None, :]
    sine_part = jnp.sin(angles)[:, None, :]
    first = entries[..., :half_width]
    second = entries[..., half_width:]
    return jnp.concatenate(
        [first * cosine - second * sine_part, second * cosine + first * sine_part], axis=-1
    )


def task_total(delta):
    return jnp.sum(delta.astype(jnp.float32), axis=0).astype(jnp.bfloat16)


def merge_weights(base, total, mixing):
    return (base.astype(jnp.float32) + mixing * total.astype(jnp.float32)).astype(jnp.bfloat16)


def on_device(
    states,
    targets,
    loss_mask,
    cand_of,
    lambdas,
    base_q,
    delta_q,
    base_k,
    delta_k,
    base_v,
    delta_v,
    base_o,
    delta_o,
    pre_gain,
    post_gain,
    final_gain,
    unembed,
):
    cand_id = lax.axis_index("cand")
    tensor_id = lax.axis_index("tensor")
    tensor_count = lax.axis_size("tensor")
    chosen = cand_of[cand_id]
    mixing = lambdas[chosen]
    group_size = tensor_count // KV
    head_start = tensor_id // group_size * HEAD_SIZE
    own_base_k = lax.dynamic_slice_in_dim(base_k, head_start, HEAD_SIZE, 1)
    own_base_v = lax.dynamic_slice_in_dim(base_v, head_start, HEAD_SIZE, 1)
    own_delta_k = lax.dynamic_slice_in_dim(delta_k, head_start, HEAD_SIZE, 2)
    own_delta_v = lax.dynamic_slice_in_dim(delta_v, head_start, HEAD_SIZE, 2)
    summed = [task_total(delta) for delta in (delta_q, own_delta_k, own_delta_v, delta_o)]
    pieces = (
        lax.all_gather(base_q, "cand", axis=0, tiled=True),
        lax.all_gather(own_base_k, "cand", axis=0, tiled=True),
        lax.all_gather(own_base_v, "cand", axis=0, tiled=True),
        lax.all_gather(base_o, "cand", axis=1, tiled=True),
        lax.all_gather(summed[0], "cand", axis=0, tiled=True),
        lax.all_gather(summed[1], "cand", axis=0, tiled=True),
        lax.all_gather(summed[2], "cand", axis=0, tiled=True),
        lax.all_gather(summed[3], "cand", axis=1, tiled=True),
    )
    base_parts = pieces[:4]
    task_parts = pieces[4:]
    w_query = merge_weights(base_parts[0], task_parts[0], mixing)
    w_key = merge_weights(base_parts[1], task_parts[1], mixing)
    w_value = merge_weights(base_parts[2], task_parts[2], mixing)
    w_out = merge_weights(base_parts[3], task_parts[3], mixing)
    length = states.shape[0]
    stream = states.astype(jnp.float32)
    normed = root_norm(stream, pre_gain).astype(jnp.bfloat16)
    query_rows = jnp.dot(normed, w_query, preferred_element_type=jnp.float32).reshape(
        length, -1, HEAD_SIZE
    )
    query_rows = rotate_pairs(query_rows, length).astype(jnp.bfloat16)
    key_full = jnp.dot(normed, w_key, preferred_element_type=jnp.float32).astype(jnp.bfloat16)
    value_full = jnp.dot(normed, w_value, preferred_element_type=jnp.float32).astype(jnp.bfloat16)
    key_matrix = rotate_pairs(
        key_full.astype(jnp.float32).reshape(length, 1, HEAD_SIZE), length
    ).astype(jnp.bfloat16)[:, 0, :]
    attention_scores = jnp.einsum(
        "lhd,md->hlm", query_rows, key_matrix, preferred_element_type=jnp.float32
    ) * HEAD_SIZE ** (-0.5)
    attention_scores = 50.0 * jnp.tanh(attention_scores / 50.0)
    causal = jnp.arange(length)[:, None] >= jnp.arange(length)[None, :]
    weights = jnp.where(causal[None, :, :], jnp.exp(attention_scores), 0.0)
    attention_probs = (weights / jnp.sum(weights, axis=-1, keepdims=True)).astype(jnp.bfloat16)
    context_rows = jnp.einsum(
        "hlm,md->lhd", attention_probs, value_full, preferred_element_type=jnp.float32
    )
    context_rows = context_rows.astype(jnp.bfloat16).reshape(length, -1)
    partial_value = jnp.dot(context_rows, w_out, preferred_element_type=jnp.float32)
    vocab_width = unembed.shape[1]
    vocab_start = (cand_id * tensor_count + tensor_id) * vocab_width
    vocab_index = jnp.arange(vocab_width)
    attended = lax.psum(partial_value, "tensor")
    final_rows = root_norm(stream + root_norm(attended, post_gain), final_gain).astype(jnp.bfloat16)
    logits = jnp.dot(
        lax.all_gather(final_rows, "cand", axis=0, tiled=True),
        unembed,
        preferred_element_type=jnp.float32,
    )
    capped = 30.0 * jnp.tanh(logits / 30.0)
    totals = jnp.sum(jnp.exp(capped), axis=1)
    local_ids = targets - vocab_start
    matches = local_ids[:, None] == vocab_index[None, :]
    picked = jnp.sum(jnp.where(matches, capped, 0.0), axis=1)
    vocab_sums = jnp.stack([totals, picked], axis=0)
    summed_terms = lax.psum(vocab_sums, ("cand", "tensor"))
    own_terms = lax.dynamic_slice_in_dim(summed_terms, cand_id * length, length, 1)
    mask_values = loss_mask.astype(jnp.float32)
    token_loss = mask_values * (jnp.log(own_terms[0]) - own_terms[1])
    onehot = (chosen == jnp.arange(CANDS)).astype(jnp.float32)
    loss_sums, counts = lax.psum(
        (onehot * jnp.sum(token_loss), onehot * jnp.sum(mask_values)), "cand"
    )
    return (token_loss, loss_sums / jnp.maximum(counts, 1.0))


def solution(mesh):
    in_specs = (
        P("cand", None),
        P(),
        P("cand"),
        P(),
        P(),
        P("cand", "tensor"),
        P(None, "cand", "tensor"),
        P("cand", None),
        P(None, "cand", None),
        P("cand", None),
        P(None, "cand", None),
        P("tensor", "cand"),
        P(None, "tensor", "cand"),
        P(),
        P(),
        P(),
        P(None, ("cand", "tensor")),
    )
    out_specs = (P("cand"), P())
    return jax.shard_map(
        on_device, mesh=mesh, in_specs=in_specs, out_specs=out_specs, check_vma=False
    )
```

profile of v0, /device:TPU:0, one launch (start us, length us, event | category | flops | bytes accessed | tf_op | source)
XLA Modules:
  0.0 451.5 jit_solution(439209231556427896)
XLA Ops:
  7.2 1.9 constant_dynamic-slice_fusion.1
  9.2 2.3 dynamic-slice_reduce_fusion
  11.6 1.6 reduce_sum.123
  13.2 0.5 all-gather.18.cloned.1.call-update
  13.8 1.8 constant_dynamic-slice_fusion.2
  15.7 2.4 dynamic-slice_reduce_fusion.1
  18.2 1.5 reduce_sum.125
  19.8 0.7 all-gather.22.cloned.1.call-update
  20.6 0.6 dynamic_slice.22
  23.1 0.6 dynamic_slice.23
  24.3 9.1 %all-gather.14.cloned.1.call-done = bf16[3584,256]{1,0:T(8,128)(2,1)} async-done(((bf16[896,256]{1,0:T(8,128)(2,1)}), bf16[3584,256]{1,0:T(8,128)(2,1)}) %all-gather.14.cloned.1.call-update) | async-done | bytes 1835024 | tf_op jit(solution)/shard_map/all_gather | solution.py:74
  33.4 22.7 %all-gather.16.cloned.1.call-done = bf16[3584,256]{1,0:T(8,128)(2,1)} async-done(((bf16[896,256]{1,0:T(8,128)(2,1)}), bf16[3584,256]{1,0:T(8,128)(2,1)}) %all-gather.16.cloned.1.call-update) | async-done | bytes 1835024 | tf_op jit(solution)/shard_map/all_gather | solution.py:78
  56.1 3.6 fusion.20
  60.0 29.2 %all-gather.20.cloned.1.call-done = bf16[3584,512]{1,0:T(8,128)(2,1)} async-done(((bf16[896,512]{1,0:T(8,128)(2,1)}), bf16[3584,512]{1,0:T(8,128)(2,1)}) %all-gather.20.cloned.1.call-update) | async-done | bytes 3670032 | tf_op jit(solution)/shard_map/all_gather | solution.py:77
  89.2 32.9 %all-gather.18.cloned.1.call-done = bf16[3584,512]{1,0:T(8,128)(2,1)} async-done(((bf16[896,512]{1,0:T(8,128)(2,1)}), bf16[3584,512]{1,0:T(8,128)(2,1)}) %all-gather.18.cloned.1.call-update) | async-done | bytes 3670032 | tf_op jit(solution)/shard_map/all_gather | solution.py:73
  122.1 5.2 %fusion = f32[128,512]{1,0:T(8,128)S(1)} fusion(bf16[3584,512]{1,0:T(8,128)(2,1)} %all-gather.20.cloned.1.call-done, bf16[3584,512]{1,0:T(8,128)(2,1)} %all-gather.18.cloned.1.call-done, f32[]{:T(128)} %bitcast.1, bf16[128,3584]{1,0:T(8,128)(2,1)S(1)} %copy-done.1, f32[3584]{0:T(1024)S(1)} %copy-done.8, f32[128]{0:T(128)S(1)} %add_rsqrt_fusion.2), kind=kOutput, calls=%fused_computation.6 | convolution fusion | flops 480772096 | bytes 8534532 | tf_op jit(solution)/shard_map/dot_general | solution.py:91
  127.9 16.7 %all-gather.10.cloned.1.call-done = bf16[3584,256]{1,0:T(8,128)(2,1)} async-done(((bf16[896,256]{1,0:T(8,128)(2,1)}), bf16[3584,256]{1,0:T(8,128)(2,1)}) %all-gather.10.cloned.1.call-update) | async-done | bytes 1835024 | tf_op jit(solution)/shard_map/all_gather | solution.py:75
  144.6 22.5 %all-gather.12.cloned.1.call-done = bf16[3584,256]{1,0:T(8,128)(2,1)} async-done(((bf16[896,256]{1,0:T(8,128)(2,1)}), bf16[3584,256]{1,0:T(8,128)(2,1)}) %all-gather.12.cloned.1.call-update) | async-done | bytes 1835024 | tf_op jit(solution)/shard_map/all_gather | solution.py:79
  167.2 3.9 convolution_convert_fusion
  171.1 29.1 %all-gather.24.cloned.1.call-done = bf16[512,3584]{1,0:T(8,128)(2,1)} async-done(((bf16[512,896]{1,0:T(8,128)(2,1)}), bf16[512,3584]{1,0:T(8,128)(2,1)}) %all-gather.24.cloned.1.call-update) | async-done | bytes 3670032 | tf_op jit(solution)/shard_map/all_gather | solution.py:80
  200.2 33.1 %all-gather.22.cloned.1.call-done = bf16[512,3584]{1,0:T(8,128)(2,1)} async-done(((bf16[512,896]{1,0:T(8,128)(2,1)}), bf16[512,3584]{1,0:T(8,128)(2,1)}) %all-gather.22.cloned.1.call-update) | async-done | bytes 3670032 | tf_op jit(solution)/shard_map/all_gather | solution.py:76
  233.3 6.6 %fusion.1 = f32[128,3584]{1,0:T(8,128)} fusion(bf16[128,512]{0,1:T(8,128)(2,1)S(1)} %bitcast.38, bf16[512,3584]{1,0:T(8,128)(2,1)} %all-gather.24.cloned.1.call-done, bf16[512,3584]{1,0:T(8,128)(2,1)} %all-gather.22.cloned.1.call-done, f32[]{:T(128)} %bitcast.1), kind=kOutput, calls=%fused_computation.7 | convolution fusion | flops 478937088 | bytes 9306116 | tf_op jit(solution)/shard_map/dot_general | solution.py:111
  240.2 95.7 %all-reduce.3.cloned.1.call-done = f32[128,3584]{1,0:T(8,128)} async-done(((f32[128,3584]{1,0:T(8,128)}), f32[128,3584]{1,0:T(8,128)}) %all-reduce.3.cloned.1.call-update) | async-done | bytes 1835024 | tf_op jit(solution)/shard_map/psum | solution.py:115
  335.9 1.8 multiply_reduce_fusion.1
  337.8 2.0 multiply_reduce_fusion
  339.8 1.4 multiply_convert_fusion
  341.3 31.1 %all-gather.26.cloned.1.call-done = bf16[512,3584]{1,0:T(8,128)(2,1)} async-done(((bf16[128,3584]{1,0:T(8,128)(2,1)}), bf16[512,3584]{1,0:T(8,128)(2,1)}) %all-gather.26.cloned.1.call-update) | async-done | bytes 3670032 | tf_op jit(solution)/shard_map/all_gather | solution.py:118
  372.4 22.9 %exponential_reduce_fusion = (f32[512]{0:T(512)S(1)}, f32[512]{0:T(512)S(1)}) fusion(s32[512]{0:T(512)S(1)} %broadcast_subtract_fusion, bf16[512,3584]{1,0:T(8,128)(2,1)} %all-gather.26.cloned.1.call-done, bf16[3584,4096]{1,0:T(8,128)(2,1)} %param.33), kind=kOutput, calls=%fused_computation.2 | convolution fusion | flops 15044968448 | bytes 33036288 | tf_op jit(solution)/shard_map/dot_general | solution.py:117
  395.3 39.3 %psum.29 = f32[2,512]{1,0:T(2,128)S(1)} all-reduce(f32[2,512]{1,0:T(2,128)S(1)} %pad_maximum_fusion), channel_id=1, replica_groups=mesh['cand'=4,'tensor'=8] {'cand','tensor'}, use_global_device_ids=true, to_apply=%region_11.12 | all-reduce | flops 1024 | bytes 8192 | tf_op jit(solution)/shard_map/psum | solution.py:128
  434.7 1.1 fusion.52
  435.8 1.8 compare_select_fusion
  437.6 6.5 %all-reduce = (f32[4]{0:T(128)S(1)}, f32[4]{0:T(128)S(1)}) all-reduce(f32[4]{0:T(128)S(1)} %get-tuple-element.18, f32[4]{0:T(128)S(1)} %get-tuple-element.17), channel_id=1, replica_groups=mesh['cand'=4,'tensor'=8] {'cand'}, use_global_device_ids=true, to_apply=%region_13.14 | all-reduce | flops 8 | bytes 64 | tf_op jit(solution)/shard_map/psum | solution.py:133
  (57 shorter events, 2.8 us)
Async XLA Ops:
  7.2 4.4 copy-start.2
  7.2 26.2 %all-gather.14.cloned.1.call-start = ((), (), s32[]{:S(2)}) async-start(), calls=%async_computation.2 | async-start | bytes 2293760 | tf_op jit(solution)/shard_map/all_gather | solution.py:74
  9.2 46.9 %all-gather.16.cloned.1.call-start = ((), (), s32[]{:S(2)}) async-start(), calls=%async_computation.3 | async-start | bytes 2293760 | tf_op jit(solution)/shard_map/all_gather | solution.py:78
  11.6 77.6 %all-gather.20.cloned.1.call-start = ((), (), s32[]{:S(2)}) async-start(), calls=%async_computation.5 | async-start | bytes 4587520 | tf_op jit(solution)/shard_map/all_gather | solution.py:77
  13.2 5.0 %copy-start.3 = (bf16[2,512,896]{2,1,0:T(8,128)(2,1)S(1)}, bf16[2,512,896]{2,1,0:T(8,128)(2,1)}, u32[]{:S(2)}) copy-start(bf16[2,512,896]{2,1,0:T(8,128)(2,1)} %param.29) | copy-start | bytes 5505028
  13.2 108.9 %all-gather.18.cloned.1.call-start = ((), (), s32[]{:S(2)}) async-start(), calls=%async_computation.4 | async-start | bytes 4587520 | tf_op jit(solution)/shard_map/all_gather | solution.py:73
  13.8 130.9 %all-gather.10.cloned.1.call-start = ((), (), s32[]{:S(2)}) async-start(), calls=%async_computation | async-start | bytes 2293760 | tf_op jit(solution)/shard_map/all_gather | solution.py:75
  15.6 4.9 %copy-start.9 = (s32[4]{0:T(128)S(1)}, s32[4]{0:T(128)}, u32[]{:S(2)}) copy-start(s32[4]{0:T(128)} %param.20) | copy-start | bytes 52
  15.6 7.4 %copy-start.10 = (f32[4]{0:T(128)S(1)}, f32[4]{0:T(128)}, u32[]{:S(2)}) copy-start(f32[4]{0:T(128)} %param.21) | copy-start | bytes 52
  15.7 8.1 %copy-start.1 = (bf16[128,3584]{1,0:T(8,128)(2,1)S(1)}, bf16[128,3584]{1,0:T(8,128)(2,1)}, u32[]{:S(2)}) copy-start(bf16[128,3584]{1,0:T(8,128)(2,1)} %param.17) | copy-start | bytes 2752516
  15.7 40.4 %copy-start.8 = (f32[3584]{0:T(1024)S(1)}, f32[3584]{0:T(1024)}, u32[]{:S(2)}) copy-start(f32[3584]{0:T(1024)} %param.30) | copy-start | bytes 43012
  15.7 151.5 %all-gather.12.cloned.1.call-start = ((), (), s32[]{:S(2)}) async-start(), calls=%async_computation.1 | async-start | bytes 2293760 | tf_op jit(solution)/shard_map/all_gather | solution.py:79
  18.2 182.1 %all-gather.24.cloned.1.call-start = ((), (), s32[]{:S(2)}) async-start(), calls=%async_computation.7 | async-start | bytes 4587520 | tf_op jit(solution)/shard_map/all_gather | solution.py:80
  19.7 213.6 %all-gather.22.cloned.1.call-start = ((), (), s32[]{:S(2)}) async-start(), calls=%async_computation.6 | async-start | bytes 4587520 | tf_op jit(solution)/shard_map/all_gather | solution.py:76
  20.5 315.4 %all-reduce.3.cloned.1.call-start = ((), (), s32[]{:S(2)}) async-start(), calls=%async_computation.8 | async-start | bytes 3670016 | tf_op jit(solution)/shard_map/psum | solution.py:115
  239.9 97.8 %copy-start.4 = (f32[3584]{0:T(1024)S(1)}, f32[3584]{0:T(1024)}, u32[]{:S(2)}) copy-start(f32[3584]{0:T(1024)} %param.31) | copy-start | bytes 43012
  239.9 99.9 %copy-start.5 = (f32[3584]{0:T(1024)S(1)}, f32[3584]{0:T(1024)}, u32[]{:S(2)}) copy-start(f32[3584]{0:T(1024)} %param.32) | copy-start | bytes 43012
  239.9 132.5 %all-gather.26.cloned.1.call-start = ((), (), s32[]{:S(2)}) async-start(), calls=%async_computation.9 | async-start | bytes 4587520 | tf_op jit(solution)/shard_map/all_gather | solution.py:118
  335.9 3.9 copy-start
  337.8 3.5 copy-start.6
  341.3 93.4 %copy-start.7 = (s32[128]{0:T(128)S(1)}, s32[128]{0:T(128)}, u32[]{:S(2)}) copy-start(s32[128]{0:T(128)} %param.19) | copy-start | bytes 1540
Sparse Core Ops, SparseCore 0:
  9.5 23.8 all-gather.13
  35.0 21.0 all-gather.15
  57.7 31.4 all-gather.19
  90.6 31.4 all-gather.17
  123.5 21.0 all-gather.9
  146.1 21.0 all-gather.11
  168.7 31.4 all-gather.23
  201.8 31.4 all-gather.21
  240.1 95.7 all-reduce.2
  341.4 30.9 all-gather.25
where the time goes:
time: 452 us
  waiting for transfers between devices  324 us (72%)
  blocking collectives  45.9 us (10%)
  matrix products  42.5 us (9%)
  other arithmetic  17.5 us (4%)
  between operations  16.3 us (4%)
  local copies, waits for them, and re-layouts  5.26 us (1%)
    psum x1, waiting for transfers between devices, on_device(): attended = lax.psum(partial_value, 'tensor')  95.7 us
    psum x1, blocking collectives, on_device(): summed_terms = lax.psum(vocab_sums, ('cand', 'tensor'))  39.3 us
    all_gather x1, waiting for transfers between devices, on_device(): lax.all_gather(base_o, 'cand', axis=1, tiled=True)  33.1 us
    all_gather x1, waiting for transfers between devices, on_device(): lax.all_gather(base_q, 'cand', axis=0, tiled=True)  32.9 us
    all_gather x1, waiting for transfers between devices, on_device(): lax.all_gather(final_rows, 'cand', axis=0, tiled=True)  31.1 us
    all_gather x1, waiting for transfers between devices, on_device(): lax.all_gather(summed[0], 'cand', axis=0, tiled=True)  29.2 us
    all_gather x1, waiting for transfers between devices, on_device(): lax.all_gather(summed[3], 'cand', axis=1, tiled=True)  29.1 us
    dot_general x1, matrix products, on_device(): jnp.dot(lax.all_gather(final_rows, 'cand', axis=0, tiled=True), unembed,...  22.9 us
  transfers between devices with their start and end apart: 10, of which 10 were waited for; matrix products, arithmetic and copies ran while one was open for 6% of the time, Pallas kernels for 0%

commit v1 on v0

--- a/solution.py
+++ b/solution.py
@@ -112,7 +112,10 @@
     vocab_width = unembed.shape[1]
     vocab_start = (cand_id * tensor_count + tensor_id) * vocab_width
     vocab_index = jnp.arange(vocab_width)
-    attended = lax.psum(partial_value, "tensor")
+    nd = lax.axis_size("tensor")
+    attended = partial_value
+    for w in [[(d, d ^ k0) for d in range(nd)] for k0 in (1, 2, 4, 8, 16) if k0 < nd]:
+        attended = attended + lax.ppermute(attended, axis_name="tensor", perm=w)
     final_rows = root_norm(stream + root_norm(attended, post_gain), final_gain).astype(jnp.bfloat16)
     logits = jnp.dot(
         lax.all_gather(final_rows, "cand", axis=0, tiled=True),

time: 452 us -> 517 us (1.14)
  waiting for transfers between devices: 324 us -> 387 us
  starting transfers between devices: 0.59 us -> 5.93 us
    ppermute x0 -> x3, waiting for transfers between devices: none -> 159 us  [on_device(): attended = attended + lax.ppermute(attended, axis_name='tensor', perm=w)]
    psum x1 -> x0, waiting for transfers between devices: 95.7 us -> none  [on_device(): attended = lax.psum(partial_value, 'tensor')]
    ppermute x0 -> x3, starting transfers between devices: none -> 5.56 us  [on_device(): attended = attended + lax.ppermute(attended, axis_name='tensor', perm=w)]
  transfers between devices with their start and end apart: 10 -> 12, of which waited for: 10 -> 12; matrix products, arithmetic and copies ran while one was open for 6% -> 5% of each run, Pallas kernels for 0% -> 0%
where the time goes in v1:
time: 517 us; the launch traced here: 516 us
  waiting for transfers between devices  387 us (75%)
  blocking collectives  45.9 us (9%)
  matrix products  41.1 us (8%)
  between operations  16.1 us (3%)
  other arithmetic  14.8 us (3%)
  starting transfers between devices  5.93 us (1%)
  local copies, waits for them, and re-layouts  5.54 us (1%)
    ppermute x3, waiting for transfers between devices, on_device(): attended = attended + lax.ppermute(attended, axis_name='tensor', perm=w)  159 us
    psum x1, blocking collectives, on_device(): summed_terms = lax.psum(vocab_sums, ('cand', 'tensor'))  39.3 us
    all_gather x1, waiting for transfers between devices, on_device(): lax.all_gather(base_o, 'cand', axis=1, tiled=True)  33.1 us
    all_gather x1, waiting for transfers between devices, on_device(): lax.all_gather(base_q, 'cand', axis=0, tiled=True)  32.9 us
    all_gather x1, waiting for transfers between devices, on_device(): lax.all_gather(final_rows, 'cand', axis=0, tiled=True)  31.6 us
    all_gather x1, waiting for transfers between devices, on_device(): lax.all_gather(summed[0], 'cand', axis=0, tiled=True)  29.2 us
    all_gather x1, waiting for transfers between devices, on_device(): lax.all_gather(summed[3], 'cand', axis=1, tiled=True)  29.1 us
    dot_general x1, matrix products, on_device(): jnp.dot(lax.all_gather(final_rows, 'cand', axis=0, tiled=True), unembed,...  22.9 us
  transfers between devices with their start and end apart: 12, of which 12 were waited for; matrix products, arithmetic and copies ran while one was open for 5% of the time, Pallas kernels for 0%

profile of v1, /device:TPU:0, one launch (start us, length us, event | category | flops | bytes accessed | tf_op | source)
XLA Modules:
  0.0 516.3 jit_solution(12674367356437719448)
XLA Ops:
  7.2 1.9 constant_dynamic-slice_fusion.1
  9.2 2.3 dynamic-slice_reduce_fusion
  11.6 1.6 reduce_sum.123
  13.8 2.0 constant_dynamic-slice_fusion.2
  15.8 2.3 dynamic-slice_reduce_fusion.1
  18.2 1.5 reduce_sum.125
  19.8 0.7 all-gather.22.cloned.1.call-update
  24.4 9.0 %all-gather.14.cloned.1.call-done = bf16[3584,256]{1,0:T(8,128)(2,1)} async-done(((bf16[896,256]{1,0:T(8,128)(2,1)}), bf16[3584,256]{1,0:T(8,128)(2,1)}) %all-gather.14.cloned.1.call-update) | async-done | bytes 1835024 | tf_op jit(solution)/shard_map/all_gather | solution.py:74
  33.4 22.7 %all-gather.16.cloned.1.call-done = bf16[3584,256]{1,0:T(8,128)(2,1)} async-done(((bf16[896,256]{1,0:T(8,128)(2,1)}), bf16[3584,256]{1,0:T(8,128)(2,1)}) %all-gather.16.cloned.1.call-update) | async-done | bytes 1835024 | tf_op jit(solution)/shard_map/all_gather | solution.py:78
  56.1 3.6 fusion.20
  60.0 29.2 %all-gather.20.cloned.1.call-done = bf16[3584,512]{1,0:T(8,128)(2,1)} async-done(((bf16[896,512]{1,0:T(8,128)(2,1)}), bf16[3584,512]{1,0:T(8,128)(2,1)}) %all-gather.20.cloned.1.call-update) | async-done | bytes 3670032 | tf_op jit(solution)/shard_map/all_gather | solution.py:77
  89.2 32.9 %all-gather.18.cloned.1.call-done = bf16[3584,512]{1,0:T(8,128)(2,1)} async-done(((bf16[896,512]{1,0:T(8,128)(2,1)}), bf16[3584,512]{1,0:T(8,128)(2,1)}) %all-gather.18.cloned.1.call-update) | async-done | bytes 3670032 | tf_op jit(solution)/shard_map/all_gather | solution.py:73
  122.1 5.2 %fusion = f32[128,512]{1,0:T(8,128)S(1)} fusion(bf16[3584,512]{1,0:T(8,128)(2,1)} %all-gather.20.cloned.1.call-done, bf16[3584,512]{1,0:T(8,128)(2,1)} %all-gather.18.cloned.1.call-done, f32[]{:T(128)} %bitcast.1, bf16[128,3584]{1,0:T(8,128)(2,1)S(1)} %copy-done, f32[3584]{0:T(1024)S(1)} %copy-done.7, f32[128]{0:T(128)S(1)} %add_rsqrt_fusion.2), kind=kOutput, calls=%fused_computation.6 | convolution fusion | flops 480772096 | bytes 8534532 | tf_op jit(solution)/shard_map/dot_general | solution.py:91
  127.9 16.8 %all-gather.10.cloned.1.call-done = bf16[3584,256]{1,0:T(8,128)(2,1)} async-done(((bf16[896,256]{1,0:T(8,128)(2,1)}), bf16[3584,256]{1,0:T(8,128)(2,1)}) %all-gather.10.cloned.1.call-update) | async-done | bytes 1835024 | tf_op jit(solution)/shard_map/all_gather | solution.py:75
  144.6 22.5 %all-gather.12.cloned.1.call-done = bf16[3584,256]{1,0:T(8,128)(2,1)} async-done(((bf16[896,256]{1,0:T(8,128)(2,1)}), bf16[3584,256]{1,0:T(8,128)(2,1)}) %all-gather.12.cloned.1.call-update) | async-done | bytes 1835024 | tf_op jit(solution)/shard_map/all_gather | solution.py:79
  167.2 3.9 convolution_convert_fusion
  171.1 29.1 %all-gather.24.cloned.1.call-done = bf16[512,3584]{1,0:T(8,128)(2,1)} async-done(((bf16[512,896]{1,0:T(8,128)(2,1)}), bf16[512,3584]{1,0:T(8,128)(2,1)}) %all-gather.24.cloned.1.call-update) | async-done | bytes 3670032 | tf_op jit(solution)/shard_map/all_gather | solution.py:80
  200.2 33.1 %all-gather.22.cloned.1.call-done = bf16[512,3584]{1,0:T(8,128)(2,1)} async-done(((bf16[512,896]{1,0:T(8,128)(2,1)}), bf16[512,3584]{1,0:T(8,128)(2,1)}) %all-gather.22.cloned.1.call-update) | async-done | bytes 3670032 | tf_op jit(solution)/shard_map/all_gather | solution.py:76
  233.3 5.3 %fusion.1 = f32[128,3584]{1,0:T(8,128)S(1)} fusion(bf16[128,512]{0,1:T(8,128)(2,1)S(1)} %bitcast.38, bf16[512,3584]{1,0:T(8,128)(2,1)} %all-gather.24.cloned.1.call-done, bf16[512,3584]{1,0:T(8,128)(2,1)} %all-gather.22.cloned.1.call-done, f32[]{:T(128)} %bitcast.1), kind=kOutput, calls=%fused_computation.7 | convolution fusion | flops 478937088 | bytes 9306116 | tf_op jit(solution)/shard_map/dot_general | solution.py:111
  238.6 1.5 collective-permute-start
  240.1 40.7 %collective-permute-done = f32[128,3584]{1,0:T(8,128)S(1)} collective-permute-done((f32[128,3584]{1,0:T(8,128)S(1)}, f32[128,3584]{1,0:T(8,128)S(1)}, u32[]{:S(2)}, u32[]{:S(2)}) %collective-permute-start) | collective-permute-done | bytes 1835040 | tf_op jit(solution)/shard_map/ppermute | solution.py:118
  281.0 1.6 collective-permute-start.1
  282.6 39.8 %collective-permute-done.1 = f32[128,3584]{1,0:T(8,128)S(1)} collective-permute-done((f32[128,3584]{1,0:T(8,128)S(1)}, f32[128,3584]{1,0:T(8,128)S(1)}, u32[]{:S(2)}, u32[]{:S(2)}) %collective-permute-start.1) | collective-permute-done | bytes 1835040 | tf_op jit(solution)/shard_map/ppermute | solution.py:118
  322.6 2.5 collective-permute-start.2
  325.0 78.2 %collective-permute-done.2 = f32[128,3584]{1,0:T(8,128)S(1)} collective-permute-done((f32[128,3584]{1,0:T(8,128)S(1)}, f32[128,3584]{1,0:T(8,128)S(1)}, u32[]{:S(2)}, u32[]{:S(2)}) %collective-permute-start.2) | collective-permute-done | bytes 1835040 | tf_op jit(solution)/shard_map/ppermute | solution.py:118
  404.3 1.4 multiply_convert_fusion
  405.8 31.6 %all-gather.26.cloned.1.call-done = bf16[512,3584]{1,0:T(8,128)(2,1)} async-done(((bf16[128,3584]{1,0:T(8,128)(2,1)}), bf16[512,3584]{1,0:T(8,128)(2,1)}) %all-gather.26.cloned.1.call-update) | async-done | bytes 3670032 | tf_op jit(solution)/shard_map/all_gather | solution.py:121
  437.4 22.9 %exponential_reduce_fusion = (f32[512]{0:T(512)S(1)}, f32[512]{0:T(512)S(1)}) fusion(s32[512]{0:T(512)S(1)} %broadcast_subtract_fusion, bf16[512,3584]{1,0:T(8,128)(2,1)} %all-gather.26.cloned.1.call-done, bf16[3584,4096]{1,0:T(8,128)(2,1)} %param.33), kind=kOutput, calls=%fused_computation.2 | convolution fusion | flops 15044968448 | bytes 33036288 | tf_op jit(solution)/shard_map/dot_general | solution.py:120
  460.3 39.3 %psum.21 = f32[2,512]{1,0:T(2,128)S(1)} all-reduce(f32[2,512]{1,0:T(2,128)S(1)} %pad_maximum_fusion), channel_id=1, replica_groups=mesh['cand'=4,'tensor'=8] {'cand','tensor'}, use_global_device_ids=true, to_apply=%region_10.11 | all-reduce | flops 1024 | bytes 8192 | tf_op jit(solution)/shard_map/psum | solution.py:131
  499.6 1.2 fusion.52
  500.8 1.9 compare_select_fusion
  502.7 6.5 %all-reduce = (f32[4]{0:T(128)S(1)}, f32[4]{0:T(128)S(1)}) all-reduce(f32[4]{0:T(128)S(1)} %get-tuple-element.20, f32[4]{0:T(128)S(1)} %get-tuple-element.19), channel_id=1, replica_groups=mesh['cand'=4,'tensor'=8] {'cand'}, use_global_device_ids=true, to_apply=%region_12.13 | all-reduce | flops 8 | bytes 64 | tf_op jit(solution)/shard_map/psum | solution.py:136
  (60 shorter events, 5.6 us)
Async XLA Ops:
  7.2 4.4 copy-start.1
  7.2 26.2 %all-gather.14.cloned.1.call-start = ((), (), s32[]{:S(2)}) async-start(), calls=%async_computation.2 | async-start | bytes 2293760 | tf_op jit(solution)/shard_map/all_gather | solution.py:74
  9.2 46.9 %all-gather.16.cloned.1.call-start = ((), (), s32[]{:S(2)}) async-start(), calls=%async_computation.3 | async-start | bytes 2293760 | tf_op jit(solution)/shard_map/all_gather | solution.py:78
  11.5 77.6 %all-gather.20.cloned.1.call-start = ((), (), s32[]{:S(2)}) async-start(), calls=%async_computation.5 | async-start | bytes 4587520 | tf_op jit(solution)/shard_map/all_gather | solution.py:77
  13.2 108.9 %all-gather.18.cloned.1.call-start = ((), (), s32[]{:S(2)}) async-start(), calls=%async_computation.4 | async-start | bytes 4587520 | tf_op jit(solution)/shard_map/all_gather | solution.py:73
  13.7 4.5 copy-start.2
  13.8 130.9 %all-gather.10.cloned.1.call-start = ((), (), s32[]{:S(2)}) async-start(), calls=%async_computation | async-start | bytes 2293760 | tf_op jit(solution)/shard_map/all_gather | solution.py:75
  15.8 151.4 %all-gather.12.cloned.1.call-start = ((), (), s32[]{:S(2)}) async-start(), calls=%async_computation.1 | async-start | bytes 2293760 | tf_op jit(solution)/shard_map/all_gather | solution.py:79
  18.1 2.4 copy-start.8
  18.2 5.0 copy-start.9
  18.2 5.6 %copy-start = (bf16[128,3584]{1,0:T(8,128)(2,1)S(1)}, bf16[128,3584]{1,0:T(8,128)(2,1)}, u32[]{:S(2)}) copy-start(bf16[128,3584]{1,0:T(8,128)(2,1)} %param.17) | copy-start | bytes 2752516
  18.2 182.1 %all-gather.24.cloned.1.call-start = ((), (), s32[]{:S(2)}) async-start(), calls=%async_computation.7 | async-start | bytes 4587520 | tf_op jit(solution)/shard_map/all_gather | solution.py:80
  19.7 36.3 %copy-start.7 = (f32[3584]{0:T(1024)S(1)}, f32[3584]{0:T(1024)}, u32[]{:S(2)}) copy-start(f32[3584]{0:T(1024)} %param.30) | copy-start | bytes 43012
  19.8 213.5 %all-gather.22.cloned.1.call-start = ((), (), s32[]{:S(2)}) async-start(), calls=%async_computation.6 | async-start | bytes 4587520 | tf_op jit(solution)/shard_map/all_gather | solution.py:76
  20.5 416.8 %all-gather.26.cloned.1.call-start = ((), (), s32[]{:S(2)}) async-start(), calls=%async_computation.8 | async-start | bytes 4587520 | tf_op jit(solution)/shard_map/all_gather | solution.py:121
  238.6 42.2 %collective-permute-start = (f32[128,3584]{1,0:T(8,128)S(1)}, f32[128,3584]{1,0:T(8,128)S(1)}, u32[]{:S(2)}, u32[]{:S(2)}) collective-permute-start(f32[128,3584]{1,0:T(8,128)S(1)} %fusion.1), channel_id=1, source_target_pairs={{0,1},{1,0},{2,3},{3,2},{4,5},{5,4},{6,7},{7,6},{8,9},{9,8},{10,11... | collective-permute-start | bytes 5505032 | tf_op jit(solution)/shard_map/ppermute | solution.py:118
  281.0 41.4 %collective-permute-start.1 = (f32[128,3584]{1,0:T(8,128)S(1)}, f32[128,3584]{1,0:T(8,128)S(1)}, u32[]{:S(2)}, u32[]{:S(2)}) collective-permute-start(f32[128,3584]{1,0:T(8,128)S(1)} %add.89), channel_id=1, source_target_pairs={{0,2},{1,3},{2,0},{3,1},{4,6},{5,7},{6,4},{7,5},{8,10},{9,11},{10,... | collective-permute-start | bytes 5505032 | tf_op jit(solution)/shard_map/ppermute | solution.py:118
  322.6 81.1 %copy-start.3 = (f32[3584]{0:T(1024)S(1)}, f32[3584]{0:T(1024)}, u32[]{:S(2)}) copy-start(f32[3584]{0:T(1024)} %param.31) | copy-start | bytes 43012
  322.6 80.7 %collective-permute-start.2 = (f32[128,3584]{1,0:T(8,128)S(1)}, f32[128,3584]{1,0:T(8,128)S(1)}, u32[]{:S(2)}, u32[]{:S(2)}) collective-permute-start(f32[128,3584]{1,0:T(8,128)S(1)} %add.90), channel_id=1, source_target_pairs={{0,4},{1,5},{2,6},{3,7},{4,0},{5,1},{6,2},{7,3},{8,12},{9,13},{10,... | collective-permute-start | bytes 5505032 | tf_op jit(solution)/shard_map/ppermute | solution.py:118
  403.6 0.7 copy-start.4
  404.3 1.4 copy-start.5
  405.8 93.9 %copy-start.6 = (s32[128]{0:T(128)S(1)}, s32[128]{0:T(128)}, u32[]{:S(2)}) copy-start(s32[128]{0:T(128)} %param.19) | copy-start | bytes 1540
Sparse Core Ops, SparseCore 0:
  9.5 23.8 all-gather.13
  35.0 21.0 all-gather.15
  57.7 31.4 all-gather.19
  90.6 31.4 all-gather.17
  123.5 21.0 all-gather.9
  146.1 21.0 all-gather.11
  168.7 31.4 all-gather.23
  201.8 31.4 all-gather.21
  405.9 31.4 all-gather.25
